TPU v7x, 32 devices: a whole 2x2x4 slice. The times are simulated.
32 devices in a mesh: grp: 2 (over y), user: 8 (over z, core), head: 2 (over x).
Axes of the slice: x: 2, y: 2, z: 4, core: 2. Of those that a mesh axis runs over, the one named last changes fastest.
Arguments:
- cand_ids: int32 [16, 512], P(('grp', 'user')), parts along dimension 0, may hold values from 0 to 4095, as said below
- prefix_len: int32 [16], P(('grp', 'user')), parts along dimension 0, may hold values from 1 to 512
- key_cache: bfloat16 [16, 512, 1024], P(('grp', 'user'), None, 'head'), parts along dimension 0, may hold values from -6 to 6
- value_cache: bfloat16 [16, 512, 1024], P(('grp', 'user'), None, 'head'), parts along dimension 0, may hold values from -6 to 6
- item_table: bfloat16 [4096, 1024], P('user'), may hold values from -6 to 6
- w_qkvu: bfloat16 [1024, 8, 4, 128], P(None, 'head'), may hold values from -0.1875 to 0.1875
- w_out: bfloat16 [8, 128, 1024], P('head'), may hold values from -0.1875 to 0.1875
Outputs:
- scores: float32 [16, 512], P(('grp', 'user')), parts along dimension 0
There are 2 independent parts, one for each index of `grp`. A program takes and returns all parts, laid end to end along the dimension named above; an argument that names none is the same for every part. Nothing has to cross between parts.
Inputs may be any that keep to these rules, and one draw needn't show every extreme that they name: `cand_ids`: item id s * 512 + r lies in table shard s. Among the 512 candidates of each aligned block of 1 users, at most 128 lie in one table shard, and in every block some shard holds exactly 128 of them.
All inputs are finite; a program needn't handle non-finite values.
Results may differ from a plain program's by a relative error of at most 0.0095.
Values may be sent and summed in bfloat16 or wider, within the bound.
A program may use at most 64 MiB of HBM per device.

v0:
```python
import jax
import jax.numpy as jnp
from jax import lax
from jax.sharding import PartitionSpec as P


def body(cand_ids, prefix_len, key_cache, value_cache, item_table, w_qkvu, w_out):
    user_count, cand_count = cand_ids.shape
    model_width = item_table.shape[1]
    heads_here = w_qkvu.shape[1]
    head_size = w_qkvu.shape[3]
    prefix_most = key_cache.shape[1]
    score_scale = head_size ** (-0.5)
    shard_count = lax.axis_size("user")
    rows_shard = item_table.shape[0]
    item_ids = cand_ids.reshape(-1)
    row_count = item_ids.shape[0]
    capacity = 2 * row_count // shard_count
    shard_of = item_ids // rows_shard
    local_row = item_ids - shard_of * rows_shard
    one_hot = (shard_of[:, None] == jnp.arange(shard_count, dtype=jnp.int32)[None, :]).astype(
        jnp.int32
    )
    position = jnp.sum((jnp.cumsum(one_hot, axis=0) - 1) * one_hot, axis=1)
    slot_index = shard_of * capacity + position
    requests = jnp.full((shard_count * capacity,), -1, jnp.int32).at[slot_index].set(local_row)
    received = lax.all_to_all(
        requests.reshape(shard_count, capacity), "user", split_axis=0, concat_axis=0, tiled=True
    )
    safe_rows = jnp.maximum(received.reshape(-1), 0)
    looked_up = item_table[safe_rows].reshape(shard_count, capacity, model_width)
    returned = lax.all_to_all(looked_up, "user", split_axis=0, concat_axis=0, tiled=True)
    embedded = returned.reshape(-1, model_width)[slot_index]
    projected = jnp.dot(
        embedded, w_qkvu.reshape(model_width, -1), preferred_element_type=jnp.float32
    )
    activated = jax.nn.silu(projected).astype(jnp.bfloat16)
    activated = activated.reshape(user_count, cand_count, heads_here, 4, head_size)
    queries = activated[:, :, :, 0]
    own_keys = activated[:, :, :, 1]
    own_values = activated[:, :, :, 2]
    gates = activated[:, :, :, 3]
    cached_keys = key_cache.reshape(user_count, prefix_most, heads_here, head_size)
    cached_values = value_cache.reshape(user_count, prefix_most, heads_here, head_size)
    raw = jnp.einsum("uchd,uphd->uhcp", queries, cached_keys, preferred_element_type=jnp.float32)
    denominator = (prefix_len + 1).astype(jnp.float32)
    in_prefix = jnp.arange(prefix_most, dtype=jnp.int32)[None, :] < prefix_len[:, None]
    weights = jnp.where(in_prefix[:, None, None, :], jax.nn.silu(raw * score_scale), 0.0)
    weights = (weights / denominator[:, None, None, None]).astype(jnp.bfloat16)
    attended = jnp.einsum(
        "uhcp,uphd->uchd", weights, cached_values, preferred_element_type=jnp.float32
    )
    own_dot = jnp.sum(queries.astype(jnp.float32) * own_keys.astype(jnp.float32), axis=-1)
    own_weight = jax.nn.silu(own_dot * score_scale) / denominator[:, None, None]
    attended = attended + own_weight[..., None] * own_values.astype(jnp.float32)
    mean_square = jnp.mean(attended * attended, axis=-1, keepdims=True)
    gated = (attended * lax.rsqrt(mean_square + 1e-06) * gates.astype(jnp.float32)).astype(
        jnp.bfloat16
    )
    partial_value = jnp.dot(
        gated.reshape(row_count, heads_here * head_size),
        w_out.reshape(heads_here * head_size, model_width),
        preferred_element_type=jnp.float32,
    )
    col_width = model_width // lax.axis_size("head")
    head_index = lax.axis_index("head")
    summed_cols = lax.psum_scatter(
        partial_value.astype(jnp.bfloat16), "head", scatter_dimension=1, tiled=True
    ).astype(jnp.float32)
    embed_cols = lax.dynamic_slice_in_dim(embedded, head_index * col_width, col_width, 1).astype(
        jnp.float32
    )
    square_part = jnp.sum(summed_cols * summed_cols, axis=1)
    inner_part = jnp.sum(summed_cols * embed_cols, axis=1)
    square_total, inner_total = lax.psum((square_part, inner_part), "head")
    scores_out = inner_total * model_width ** (-0.5) * lax.rsqrt(square_total / model_width + 1e-06)
    return scores_out.reshape(user_count, cand_count)


def solution(mesh):
    in_specs = (
        P(("grp", "user"), None),
        P(("grp", "user")),
        P(("grp", "user"), None, "head"),
        P(("grp", "user"), None, "head"),
        P("user", None),
        P(None, "head", None, None),
        P("head", None, None),
    )
    out_specs = P(("grp", "user"), None)
    return jax.shard_map(body, mesh=mesh, in_specs=in_specs, out_specs=out_specs, check_vma=False)
```

profile of v0, /device:TPU:0, one launch (start us, length us, event | category | flops | bytes accessed | tf_op | source)
XLA Modules:
  0.0 148.5 jit_solution(10480768824271647878)
XLA Ops:
  6.5 0.8 add_select_fusion
  7.3 1.1 reduce-window.6
  8.5 0.2 slice_reduce_fusion
  8.7 0.7 multiply_subtract_fusion
  9.4 0.1 fusion.12
  9.5 0.7 compare_select_fusion
  10.2 2.4 %scatter_custom_fusion = s32[1024]{0:T(1024)S(1)} fusion(s32[512]{0:T(512)S(1)} %bitcast.64, s32[512]{0:T(512)S(1)} %get-tuple-element.13, s32[]{:T(128)} %constant.19.clone.1), kind=kCustom, calls=%fused_computation.53 | custom fusion | bytes 4100 | tf_op jit(solution)/shard_map/scatter | solution.py:26
  12.7 11.7 %all_to_all.14 = s32[8,1,128]{2,1,0:T(1,128)S(1)} all-to-all(s32[8,1,128]{2,1,0:T(1,128)S(1)} %bitcast.62), channel_id=1, replica_groups=mesh['grp'=2,'user'=8,'head'=2] {'user'}, dimensions={0} | all-to-all | bytes 8192 | tf_op jit(solution)/shard_map/all_to_all | solution.py:27
  24.4 0.0 copy-done
  24.4 5.4 %gather_fusion = bf16[1024,1024]{1,0:T(8,128)(2,1)} fusion(bf16[512,1024]{1,0:T(8,128)(2,1)S(1)} %copy-done, s32[1024]{0:T(1024)S(1)} %broadcast_clamp_fusion), kind=kCustom, calls=%fused_computation | custom fusion | bytes 4198400 | tf_op jit(solution)/shard_map/gather | solution.py:31
  29.8 3.6 %all-to-all-start.1 = ((bf16[8,128,1024]{2,1,0:T(8,128)(2,1)}), bf16[8,128,1024]{2,1,0:T(8,128)(2,1)S(1)}, u32[]{:S(2)}, u32[]{:S(2)}) async-start(bf16[8,128,1024]{2,1,0:T(8,128)(2,1)} %bitcast.57), calls=%async_computation.1 | async-start | bytes 4194304 | tf_op jit(solution)/shard_map/all_to_all | solution.py:32
  33.4 0.0 reduce-scatter.2.cloned.1.call-start
  33.5 7.8 %reshape.313 = bf16[1024,2048]{1,0:T(8,128)(2,1)} reshape(bf16[1024,4,4,128]{3,2,1,0:T(4,128)(2,1)} %param.12) | data formatting | bytes 8388608 | tf_op jit(solution)/shard_map/reshape | solution.py:35
  41.9 2.0 %copy.20 = bf16[1,512,512]{1,2,0:T(8,128)(2,1)} copy(bf16[1,512,512]{2,1,0:T(8,128)(2,1)} %param.10) | data formatting | bytes 1048576 | tf_op jit(solution)/shard_map/reshape.9
  44.0 2.0 %reshape.316 = bf16[512,4,128]{2,1,0:T(4,128)(2,1)} reshape(bf16[1,512,512]{2,1,0:T(8,128)(2,1)} %param.9) | data formatting | bytes 1048576 | tf_op jit(solution)/shard_map/reshape.6
  45.9 36.4 %all-to-all-done.1 = bf16[8,128,1024]{2,1,0:T(8,128)(2,1)S(1)} async-done(((bf16[8,128,1024]{2,1,0:T(8,128)(2,1)}), bf16[8,128,1024]{2,1,0:T(8,128)(2,1)S(1)}, u32[]{:S(2)}, u32[]{:S(2)}) %all-to-all-start.1) | async-done | bytes 2097184 | tf_op jit(solution)/shard_map/all_to_all | solution.py:32
  82.4 2.8 %gather_fusion.1 = bf16[512,1024]{1,0:T(8,128)(2,1)} fusion(bf16[1024,1024]{1,0:T(8,128)(2,1)S(1)} %bitcast.56, s32[1024]{0:T(1024)S(1)} %pad_clamp_fusion), kind=kCustom, calls=%fused_computation.1 | custom fusion | bytes 2099200 | tf_op jit(solution)/shard_map/gather | solution.py:33
  85.2 6.6 %multiply_convert_fusion = bf16[512,2048]{1,0:T(8,128)(2,1)} fusion(bf16[512,1024]{1,0:T(8,128)(2,1)} %gather_fusion.1, bf16[1024,2048]{1,0:T(8,128)(2,1)} %reshape.313), kind=kOutput, calls=%fused_computation.4 | convolution fusion | flops 2152726528 | bytes 7340032 | tf_op jit(solution)/shard_map/dot_general | solution.py:34
  91.8 3.2 %reshape.314 = bf16[1,512,4,4,128]{4,3,2,1,0:T(4,128)(2,1)S(1)} reshape(bf16[512,2048]{1,0:T(8,128)(2,1)} %multiply_convert_fusion) | data formatting | bytes 4194304 | tf_op jit(solution)/shard_map/reshape | solution.py:38
  95.0 4.5 %fusion.24 = (bf16[1,512,4,1,128]{4,3,2,1,0:T(2,128)(2,1)}, bf16[1,512,4,1,128]{4,3,2,1,0:T(2,128)(2,1)}, bf16[1,512,4,1,128]{4,3,2,1,0:T(2,128)(2,1)}, bf16[1,512,4,1,128]{4,3,2,1,0:T(2,128)(2,1)}) fusion(bf16[1,512,4,4,128]{4,3,2,1,0:T(4,128)(2,1)S(1)} %reshape.314), kind=kLoop, calls=%fused_computation.61 | loop fusion | bytes 4194304 | tf_op jit(solution)/shard_map/slice | solution.py:42
  99.5 2.3 %copy.23 = bf16[1,512,4,1,128]{1,4,2,3,0:T(8,128)(2,1)S(1)} copy(bf16[1,512,4,1,128]{4,3,2,1,0:T(2,128)(2,1)} %get-tuple-element.12) | data formatting | bytes 1048576
  101.9 1.9 %multiply_reduce_fusion.1 = f32[512,4]{0,1:T(4,128)S(1)} fusion(bf16[1,512,4,1,128]{4,3,2,1,0:T(2,128)(2,1)} %get-tuple-element.10, bf16[1,512,4,1,128]{4,3,2,1,0:T(2,128)(2,1)} %get-tuple-element.11), kind=kLoop, calls=%fused_computation.17 | loop fusion | flops 1046528 | bytes 1056768 | tf_op jit(solution)/shard_map/reduce_sum | solution.py:53
  103.8 0.0 copy-start.1
  103.8 4.7 %multiply_reduce_fusion = (f32[512,4]{0,1:T(4,128)S(1)}, f32[1,512,4,128]{1,3,2,0:T(8,128)}) fusion(bf16[1,512,4,1,128]{1,4,2,3,0:T(8,128)(2,1)S(1)} %copy.23, f32[512,4]{0,1:T(4,128)S(1)} %fusion.14, bf16[512,4,128]{0,2,1:T(8,128)(2,1)} %bitcast.58, f32[]{:T(128)} %bitcast.13, pred[512]{0:T(512)(128)(4,1)S(1)} %iota_compare_fusion.2, ...), kind=kOutput, calls=%fused_computation.16 | convolution fusion | flops 546568192 | bytes 3162628 | tf_op jit(solution)/shard_map/uhcp,uphd->uchd/dot_general | solution.py:50
  108.5 2.3 %copy.24 = bf16[1,512,4,1,128]{1,4,2,3,0:T(8,128)(2,1)} copy(bf16[1,512,4,1,128]{4,3,2,1,0:T(2,128)(2,1)S(1)} %copy-done.1) | data formatting | bytes 1048576
  110.8 1.5 %fusion.5 = bf16[1,512,4,128]{1,3,2,0:T(8,128)(2,1)S(1)} fusion(f32[1,512,4,128]{1,3,2,0:T(8,128)} %get-tuple-element.16, bf16[1,512,4,1,128]{1,4,2,3,0:T(8,128)(2,1)} %copy.24, f32[512,4]{0,1:T(4,128)S(1)} %add_rsqrt_fusion), kind=kLoop, calls=%fused_computation.14 | loop fusion | flops 1048576 | bytes 2105344 | tf_op jit(solution)/shard_map/convert_element_type | solution.py:57
  112.4 2.9 %convolution_convert_fusion = bf16[512,1024]{1,0:T(8,128)(2,1)} fusion(bf16[512,512]{0,1:T(8,128)(2,1)S(1)} %bitcast.59, bf16[512,1024]{1,0:T(8,128)(2,1)} %bitcast.67), kind=kOutput, calls=%fused_computation.5 | convolution fusion | flops 537395200 | bytes 2621440 | tf_op jit(solution)/shard_map/dot_general | solution.py:60
  115.3 0.0 reduce-scatter.2.cloned.1.call-update
  115.3 19.4 %reduce-scatter.2.cloned.1.call-done = bf16[512,512]{1,0:T(8,128)(2,1)} async-done(((bf16[512,1024]{1,0:T(8,128)(2,1)}), bf16[512,512]{1,0:T(8,128)(2,1)}) %reduce-scatter.2.cloned.1.call-update) | async-done | bytes 524304 | tf_op jit(solution)/shard_map/reduce_scatter | solution.py:67
  134.8 1.3 fusion.3
  136.1 4.9 %all-reduce = (f32[512]{0:T(512)S(1)}, f32[512]{0:T(512)S(1)}) all-reduce(f32[512]{0:T(512)S(1)} %get-tuple-element.6, f32[512]{0:T(512)S(1)} %get-tuple-element.5), channel_id=1, replica_groups=mesh['grp'=2,'user'=8,'head'=2] {'head'}, use_global_device_ids=true, to_apply=%region_10.11 | all-reduce | flops 1024 | bytes 8192 | tf_op jit(solution)/shard_map/psum | solution.py:75
  141.0 0.6 rsqrt_multiply_fusion
  (13 shorter events, 0.1 us)
Async XLA Ops:
  6.5 17.9 %copy-start = (bf16[512,1024]{1,0:T(8,128)(2,1)S(1)}, bf16[512,1024]{1,0:T(8,128)(2,1)}, u32[]{:S(2)}) copy-start(bf16[512,1024]{1,0:T(8,128)(2,1)} %param.11) | copy-start | bytes 3145732
  29.8 52.6 %all-to-all-start.1 = ((bf16[8,128,1024]{2,1,0:T(8,128)(2,1)}), bf16[8,128,1024]{2,1,0:T(8,128)(2,1)S(1)}, u32[]{:S(2)}, u32[]{:S(2)}) async-start(bf16[8,128,1024]{2,1,0:T(8,128)(2,1)} %bitcast.57), calls=%async_computation.1 | async-start | bytes 4194304 | tf_op jit(solution)/shard_map/all_to_all | solution.py:32
  33.4 101.4 %reduce-scatter.2.cloned.1.call-start = ((), (), s32[]{:S(2)}) async-start(), calls=%async_computation.3 | async-start | bytes 1572864 | tf_op jit(solution)/shard_map/reduce_scatter | solution.py:67
  103.8 4.8 %copy-start.1 = (bf16[1,512,4,1,128]{4,3,2,1,0:T(2,128)(2,1)S(1)}, bf16[1,512,4,1,128]{4,3,2,1,0:T(2,128)(2,1)}, u32[]{:S(2)}) copy-start(bf16[1,512,4,1,128]{4,3,2,1,0:T(2,128)(2,1)} %get-tuple-element.9) | copy-start | bytes 1572868
  108.5 26.2 %copy-start.2 = (bf16[512,1024]{1,0:T(8,128)(2,1)S(1)}, bf16[512,1024]{1,0:T(8,128)(2,1)}, u32[]{:S(2)}) copy-start(bf16[512,1024]{1,0:T(8,128)(2,1)} %gather_fusion.1) | copy-start | bytes 3145732
Sparse Core Ops, SparseCore 0:
  115.4 19.2 reduce-scatter.1
where the time goes:
time: 149 us; the launch traced here: 148 us
  waiting for transfers between devices  55.9 us (38%)
  local copies, waits for them, and re-layouts  35 us (23%)
  blocking collectives  16.7 us (11%)
  matrix products  14.3 us (10%)
  between operations  14.1 us (9%)
  other arithmetic  8.84 us (6%)
  starting transfers between devices  3.64 us (2%)
    all_to_all x1, waiting for transfers between devices, body(): lax.all_to_all(looked_up, 'user', split_axis=0, concat_axis=0, tiled=True)  36.4 us
    reduce_scatter x1, waiting for transfers between devices, body(): lax.psum_scatter(partial_value.astype(jnp.bfloat16), 'head', scatter_dime...  19.4 us
    all_to_all x1, blocking collectives, body(): lax.all_to_all(requests.reshape(shard_count, capacity), 'user', split_axi...  11.7 us
    reshape x1, local copies, waits for them, and re-layouts, body(): w_qkvu.reshape(model_width, -1)  7.8 us
    dot_general x1, matrix products, body(): jnp.dot(embedded, w_qkvu.reshape(model_width, -1), preferred_element_type...  6.63 us
    gather x1, local copies, waits for them, and re-layouts, body(): item_table[safe_rows].reshape(shard_count, capacity, model_width)  5.37 us
    psum x1, blocking collectives, body(): square_total, inner_total = lax.psum((square_part, inner_part), 'head')  4.93 us
    dot_general x1, matrix products, body(): jnp.einsum('uhcp,uphd->uchd', weights, cached_values, preferred_element_t...  4.74 us
  transfers between devices with their start and end apart: 2, of which 2 were waited for; matrix products, arithmetic and copies ran while one was open for 8% of the time, Pallas kernels for 0%

commit v1 on v0

--- a/solution.py
+++ b/solution.py
@@ -1,7 +1,373 @@
+import functools
+
 import jax
 import jax.numpy as jnp
 from jax import lax
+from jax.experimental import pallas as pl
+from jax.experimental.pallas import tpu as pltpu
 from jax.sharding import PartitionSpec as P
+
+MESH = pl.DeviceIdType.MESH
+PIECES = 2
+
+
+def silu(v):
+    return v * (0.5 * jnp.tanh(0.5 * v) + 0.5)
+
+
+def kernel(
+    chips, prefix_ref, ids_ref, key_hbm, value_hbm, table_hbm, w_hbm, wout_hbm, out_ref,
+    tab, ids_peer, ids_wide, picked, one_hot, emb, emb_peer, w, keys, values, wout, acc, gated,
+    gated_peer, halves, local_sem, z_send, z_recv, ids_sem, exch_send, exch_recv, wout_sem, tail_sem,
+):
+    grp, user, head = lax.axis_index("grp"), lax.axis_index("user"), lax.axis_index("head")
+    z, core = user // 2, user % 2
+    sibling = user + 1 - 2 * core
+    quarter = 2 * grp + head
+    shards, rows, width = tab.shape
+    cand = ids_ref.shape[1]
+    half = cand // 2
+    piece = rows // PIECES
+    heads, head_size = wout_hbm.shape[0], wout_hbm.shape[1]
+    here = heads * head_size
+    prefix_most = keys.shape[0]
+    model = w.shape[0]
+    x_peer = (grp, user, 1 - head)
+    y_peer = (1 - grp, user, head)
+    corner = (1 - grp, user, 1 - head)
+
+    own = pltpu.make_async_copy(
+        table_hbm.at[:, pl.ds(pl.multiple_of(quarter * width, width), width)],
+        tab.at[user], local_sem.at[0],
+    )
+    loads = [
+        pltpu.make_async_copy(wout_hbm, wout.at[head], local_sem.at[1]),
+        pltpu.make_async_copy(w_hbm, w, local_sem.at[2]),
+        pltpu.make_async_copy(key_hbm.at[0], keys, local_sem.at[3]),
+        pltpu.make_async_copy(value_hbm.at[0], values, local_sem.at[4]),
+    ]
+    own.start()
+    for load in loads:
+        load.start()
+
+    barrier = pltpu.get_barrier_semaphore()
+
+    def greet(device):
+        pl.semaphore_signal(barrier, inc=1, device_id=device, device_id_type=MESH)
+
+    for device in ((grp, sibling, head), x_peer, y_peer, corner):
+        greet(device)
+
+    @pl.when(z > 0)
+    def _():
+        greet((grp, user - 2, head))
+
+    @pl.when(z < chips - 1)
+    def _():
+        greet((grp, user + 2, head))
+
+    pl.semaphore_wait(barrier, 4 + jnp.minimum(z, 1) + jnp.minimum(chips - 1 - z, 1))
+
+    def remote(src, dst, send, recv, device):
+        return pltpu.make_async_remote_copy(
+            src_ref=src, dst_ref=dst, send_sem=send, recv_sem=recv, device_id=device,
+            device_id_type=MESH,
+        )
+
+    def block(chip, parity, part):
+        return tab.at[2 * chip + parity, pl.ds(part * piece, piece)]
+
+    def along(chip, part, step):
+        place = block(chip, core, part)
+        return remote(
+            place, place, z_send.at[0 if step > 0 else 1, chip, part], z_recv.at[0, chip, part],
+            (grp, user + 2 * step, head),
+        )
+
+    def across(chip, part, parity):
+        place = block(chip, parity, part)
+        return remote(
+            place, place, z_send.at[2, chip, part], z_recv.at[1, chip, part],
+            (grp, sibling, head),
+        )
+
+    def when(condition, action):
+        pl.when(condition)(action)
+
+    ids_copy = remote(ids_ref, ids_peer, ids_sem.at[0], ids_sem.at[1], y_peer)
+    ids_copy.start()
+    own.wait()
+    for part in range(PIECES):
+        when(z < chips - 1, lambda: along(z, part, 1).start())
+        when(z > 0, lambda: along(z, part, -1).start())
+        across(z, part, core).start()
+    loads[0].wait()
+    wout_copies = []
+    depth = head_size * heads // 2
+
+    def wout_part(group, part):
+        return wout.at[group, pl.ds(pl.multiple_of(part * (heads // 2), heads // 2), heads // 2)]
+
+    to_peer = remote(wout_part(head, core), wout_part(head, core), wout_sem.at[0], wout_sem.at[1], x_peer)
+    to_peer.start()
+    ids_copy.wait()
+
+    lane = lax.broadcasted_iota(jnp.int32, (cand, 128), 1)
+    diagonal = lax.broadcasted_iota(jnp.int32, (cand, cand), 0) == lax.broadcasted_iota(
+        jnp.int32, (cand, cand), 1
+    )
+    for which, source in enumerate((ids_ref, ids_peer)):
+        column = jnp.sum(
+            jnp.where(diagonal, source[...].astype(jnp.float32), 0.0), axis=1, keepdims=True
+        ).astype(jnp.int32)
+        ids_wide[which] = jnp.broadcast_to(column, (cand, 128))
+    picked[...] = jnp.zeros_like(picked)
+
+    def pick(chip):
+        def step(i, carry):
+            which, parity = i // 2, i % 2
+            shard = 2 * chip + parity
+            wide = ids_wide[which] - shard * rows
+            for j in range(rows // 128):
+                one_hot[:, j * 128 : (j + 1) * 128] = jnp.where(
+                    wide == lane + j * 128, 1.0, 0.0
+                ).astype(jnp.bfloat16)
+            picked[which] += jnp.dot(
+                one_hot[...], tab[shard], preferred_element_type=jnp.float32
+            )
+            return carry
+
+        lax.fori_loop(0, 4, step, 0)
+
+    def take(chip):
+        for part in range(PIECES):
+            across(chip, part, 1 - core).wait_recv()
+        pick(chip)
+
+    take(z)
+    for distance in range(1, chips):
+        for part in range(PIECES):
+
+            @pl.when(z - distance >= 0)
+            def _():
+                along(z - distance, part, 1).wait_recv()
+                when(z < chips - 1, lambda: along(z - distance, part, 1).start())
+                across(z - distance, part, core).start()
+
+            @pl.when(z + distance < chips)
+            def _():
+                along(z + distance, part, -1).wait_recv()
+                when(z > 0, lambda: along(z + distance, part, -1).start())
+                across(z + distance, part, core).start()
+
+        when(z - distance >= 0, lambda: take(z - distance))
+        when(z + distance < chips, lambda: take(z + distance))
+
+    emb[quarter] = picked[0].astype(jnp.bfloat16)
+    emb_peer[...] = picked[1].astype(jnp.bfloat16)
+    exchange = [
+        remote(emb.at[quarter], emb.at[quarter], exch_send.at[0], exch_recv.at[quarter], x_peer),
+        remote(emb_peer, emb.at[quarter], exch_send.at[1], exch_recv.at[quarter], y_peer),
+        remote(emb_peer, emb.at[quarter], exch_send.at[2], exch_recv.at[quarter], corner),
+    ]
+    for copy in exchange:
+        copy.start()
+    to_peer.wait()
+    forward = remote(
+        wout_part(1 - head, core), wout_part(1 - head, core), wout_sem.at[2], wout_sem.at[3],
+        (grp, sibling, head),
+    )
+    forward.start()
+    for load in loads[1:]:
+        load.wait()
+
+    def weight(which, h):
+        return w[
+            pl.ds(pl.multiple_of(which * width, width), width),
+            pl.ds(pl.multiple_of(h * 4 * head_size, 4 * head_size), 4 * head_size),
+        ]
+
+    def embedded(which, r):
+        return emb[which, pl.ds(pl.multiple_of(r * half, half), half)]
+
+    def project(which, r, h):
+        return jnp.dot(embedded(which, r), weight(which, h), preferred_element_type=jnp.float32)
+
+    def arrived(which):
+        remote(
+            emb.at[which], emb.at[which], exch_send.at[0], exch_recv.at[which], x_peer
+        ).wait_recv()
+
+    x_quarter, y_quarter = 2 * grp + 1 - head, 2 * (1 - grp) + head
+    corner_quarter = 2 * (1 - grp) + 1 - head
+
+    def first(i, carry):
+        acc[i // heads, i % heads] = project(quarter, i // heads, i % heads)
+        return carry
+
+    lax.fori_loop(0, 2 * heads, first, 0)
+    for which in (x_quarter, y_quarter):
+        arrived(which)
+
+        def add(i, carry):
+            acc[i // heads, i % heads] += project(which, i // heads, i % heads)
+            return carry
+
+        lax.fori_loop(0, 2 * heads, add, 0)
+    arrived(corner_quarter)
+
+    length = prefix_ref[0]
+    inverse = 1.0 / (length + 1).astype(jnp.float32)
+    in_prefix = lax.broadcasted_iota(jnp.int32, (1, prefix_most), 1) < length
+    factor = jnp.where(in_prefix, inverse, 0.0)
+    scale = head_size ** (-0.5)
+
+    def attend(r):
+        def step(h, carry):
+            activated = silu(acc[r, h] + project(corner_quarter, r, h)).astype(jnp.bfloat16)
+            query, own_key, own_value, gate = (
+                activated[:, j * head_size : (j + 1) * head_size] for j in range(4)
+            )
+            columns = pl.ds(pl.multiple_of(h * head_size, head_size), head_size)
+            raw = lax.dot_general(
+                query, keys[:, columns], (((1,), (1,)), ((), ())),
+                preferred_element_type=jnp.float32,
+            )
+            weights = (silu(raw * scale) * factor).astype(jnp.bfloat16)
+            attended = jnp.dot(weights, values[:, columns], preferred_element_type=jnp.float32)
+            own_dot = jnp.sum(
+                query.astype(jnp.float32) * own_key.astype(jnp.float32), axis=1, keepdims=True
+            )
+            attended += silu(own_dot * scale) * inverse * own_value.astype(jnp.float32)
+            mean_square = jnp.mean(attended * attended, axis=1, keepdims=True)
+            gated[r, :, columns] = (
+                attended * lax.rsqrt(mean_square + 1e-06) * gate.astype(jnp.float32)
+            ).astype(jnp.bfloat16)
+            return carry
+
+        lax.fori_loop(0, heads, step, 0)
+
+    attend(1 - head)
+    hand_over = remote(gated.at[1 - head], gated_peer, tail_sem.at[0], tail_sem.at[1], x_peer)
+    hand_over.start()
+    attend(head)
+    forward.wait()
+
+    def product(rows_here, group):
+        return (
+            jnp.dot(
+                rows_here, wout[group].reshape(here, model), preferred_element_type=jnp.float32
+            )
+            .astype(jnp.bfloat16)
+            .astype(jnp.float32)
+        )
+
+    summed = product(gated[head], head)
+    hand_over.wait()
+    summed += product(gated_peer[...], 1 - head)
+    square = jnp.sum(summed * summed, axis=1, keepdims=True)
+    inner = sum(
+        jnp.sum(
+            summed[:, i * width : (i + 1) * width] * embedded(i, head).astype(jnp.float32),
+            axis=1, keepdims=True,
+        )
+        for i in range(model // width)
+    )
+    score = inner * model ** (-0.5) * lax.rsqrt(square / model + 1e-06)
+    halves[head] = jnp.sum(jnp.where(diagonal[:half, :half], score, 0.0), axis=0, keepdims=True)
+    last = remote(halves.at[head], halves.at[head], tail_sem.at[2], tail_sem.at[3], x_peer)
+    last.start()
+    for part in range(PIECES):
+        for chip in range(chips):
+
+            @pl.when(z < chips - 1)
+            def _():
+                when(chip <= z, lambda: along(chip, part, 1).wait_send())
+
+            @pl.when(z > 0)
+            def _():
+                when(chip >= z, lambda: along(chip, part, -1).wait_send())
+
+            across(chip, part, core).wait_send()
+    for copy in exchange:
+        copy.wait_send()
+    last.wait()
+    for i in range(2):
+        out_ref[:, i * half : (i + 1) * half] = halves[i]
+
+
+def fused_body(mesh, cand_ids, prefix_len, key_cache, value_cache, item_table, w_qkvu, w_out):
+    cand = cand_ids.shape[1]
+    rows, model = item_table.shape
+    heads, head_size = w_qkvu.shape[1], w_qkvu.shape[3]
+    prefix_most, here = key_cache.shape[1:]
+    shards = mesh.shape["user"]
+    chips = shards // 2
+    width = model // 4
+    half = cand // 2
+    hbm = pl.BlockSpec(memory_space=pl.ANY)
+    bf16, f32 = jnp.bfloat16, jnp.float32
+    return pl.pallas_call(
+        functools.partial(kernel, chips),
+        out_shape=jax.ShapeDtypeStruct((1, cand), f32),
+        in_specs=[
+            pl.BlockSpec(memory_space=pltpu.SMEM), pl.BlockSpec(memory_space=pltpu.VMEM),
+            hbm, hbm, hbm, hbm, hbm,
+        ],
+        out_specs=pl.BlockSpec(memory_space=pltpu.VMEM),
+        scratch_shapes=[
+            pltpu.VMEM((shards, rows, width), bf16),
+            pltpu.VMEM((1, cand), jnp.int32),
+            pltpu.VMEM((2, cand, 128), jnp.int32),
+            pltpu.VMEM((2, cand, width), f32),
+            pltpu.VMEM((cand, rows), bf16),
+            pltpu.VMEM((4, cand, width), bf16),
+            pltpu.VMEM((cand, width), bf16),
+            pltpu.VMEM((model, heads * 4 * head_size), bf16),
+            pltpu.VMEM((prefix_most, here), bf16),
+            pltpu.VMEM((prefix_most, here), bf16),
+            pltpu.VMEM((2, heads, head_size, model), bf16),
+            pltpu.VMEM((2, heads, half, 4 * head_size), f32),
+            pltpu.VMEM((2, half, here), bf16),
+            pltpu.VMEM((half, here), bf16),
+            pltpu.VMEM((2, 1, half), f32),
+            pltpu.SemaphoreType.DMA((5,)),
+            pltpu.SemaphoreType.DMA((3, chips, PIECES)),
+            pltpu.SemaphoreType.DMA((2, chips, PIECES)),
+            pltpu.SemaphoreType.DMA((2,)),
+            pltpu.SemaphoreType.DMA((3,)),
+            pltpu.SemaphoreType.DMA((4,)),
+            pltpu.SemaphoreType.DMA((4,)),
+            pltpu.SemaphoreType.DMA((4,)),
+        ],
+        compiler_params=pltpu.CompilerParams(
+            collective_id=0, has_side_effects=True, vmem_limit_bytes=60 * 1024 * 1024
+        ),
+    )(
+        prefix_len, cand_ids, key_cache, value_cache, item_table,
+        w_qkvu.reshape(model, heads * 4 * head_size), w_out,
+    )
+
+
+def fits_fused(mesh):
+    shape = mesh.shape
+    return shape["grp"] == 2 and shape["head"] == 2 and shape["user"] % 2 == 0 and shape["user"] <= 8
+
+
+def fused(mesh):
+    in_specs = (
+        P(("grp", "user"), None),
+        P(("grp", "user")),
+        P(("grp", "user"), None, "head"),
+        P(("grp", "user"), None, "head"),
+        P("user", None),
+        P(None, "head", None, None),
+        P("head", None, None),
+    )
+    return jax.shard_map(
+        functools.partial(fused_body, mesh), mesh=mesh, in_specs=in_specs,
+        out_specs=P(("grp", "user"), None), check_vma=False,
+    )
 
 
 def body(cand_ids, prefix_len, key_cache, value_cache, item_table, w_qkvu, w_out):
@@ -78,6 +444,8 @@
 
 
 def solution(mesh):
+    if fits_fused(mesh):
+        return fused(mesh)
     in_specs = (
         P(("grp", "user"), None),
         P(("grp", "user")),

time: 149 us -> 64.5 us (0.43)
  waiting for transfers between devices: 55.9 us -> 0 us
  Pallas kernels: 0 us -> 54.5 us
  local copies, waits for them, and re-layouts: 35 us -> 9.05 us
  blocking collectives: 16.7 us -> 0 us
  matrix products: 14.3 us -> 0 us
  between operations: 14.1 us -> 0.66 us
  other arithmetic: 8.84 us -> 0 us
  starting transfers between devices: 3.64 us -> 0 us
    pallas_call x0 -> x1, Pallas kernels: none -> 54.5 us  [fused_body(): pl.pallas_call(functools.partial(kernel, chips), out_shape=jax.ShapeDtype...]
    all_to_all x1 -> x0, waiting for transfers between devices: 36.4 us -> none  [body(): lax.all_to_all(looked_up, 'user', split_axis=0, concat_axis=0, tiled=True)]
    reduce_scatter x1 -> x0, waiting for transfers between devices: 19.4 us -> none  [body(): lax.psum_scatter(partial_value.astype(jnp.bfloat16), 'head', scatter_dime...]
    dot_general x3 -> x0, matrix products: 14.3 us -> none  [the longest x1 6.63 us: body(): jnp.dot(embedded, w_qkvu.reshape(model_width, -1), preferred_element_type...]
    all_to_all x1 -> x0, blocking collectives: 11.7 us -> none  [body(): lax.all_to_all(requests.reshape(shard_count, capacity), 'user', split_axi...]
    gather x2 -> x0, local copies, waits for them, and re-layouts: 8.16 us -> none  [the longest x1 5.37 us: body(): item_table[safe_rows].reshape(shard_count, capacity, model_width)]
    psum x1 -> x0, blocking collectives: 4.93 us -> none  [body(): square_total, inner_total = lax.psum((square_part, inner_part), 'head')]
    slice x2 -> x0, local copies, waits for them, and re-layouts: 4.7 us -> none  [the longest x1 4.48 us: body(): gates = activated[:, :, :, 3]]
  transfers between devices with their start and end apart: 2 -> 0, of which waited for: 2 -> 0; matrix products, arithmetic and copies ran while one was open for 8% -> 0% of each run, Pallas kernels for 0% -> 0%
where the time goes in v1:
time: 64.5 us; the launch traced here: 64.2 us
  Pallas kernels  54.5 us (84%)
  local copies, waits for them, and re-layouts  9.05 us (14%)
  between operations  0.66 us (1%)
    pallas_call x1, Pallas kernels, fused_body(): pl.pallas_call(functools.partial(kernel, chips), out_shape=jax.ShapeDtype...  54.5 us
    reshape x1, local copies, waits for them, and re-layouts, fused_body(): w_qkvu.reshape(model, heads * 4 * head_size)  7.8 us

profile of v1, /device:TPU:0, one launch (start us, length us, event | category | flops | bytes accessed | tf_op | source)
XLA Modules:
  0.0 64.2 jit_solution(12817414973881593451)
XLA Ops:
  0.7 7.8 %reshape.3.w_hbm = bf16[1024,2048]{1,0:T(8,128)(2,1)} reshape(bf16[1024,4,4,128]{3,2,1,0:T(4,128)(2,1)} %param.12) | data formatting | bytes 8388608 | tf_op jit(solution)/shard_map/reshape | solution.py:348
  8.5 54.5 %shard_map.73 = f32[1,512]{1,0:T(1,128)} custom-call(s32[1]{0:T(128)S(6)} %copy.9.prefix_ref, s32[1,512]{1,0:T(1,128)} %ids_ref.1, bf16[1,512,512]{2,1,0:T(8,128)(2,1)} %key_hbm.1, bf16[1,512,512]{2,1,0:T(8,128)(2,1)} %value_hbm.1, bf16[512,1024]{1,0:T(8,128)(2,1)} %table_hbm.1, bf16[1024,2048]{1,0:T(8,128)(2,1)} %reshape.3.w_hbm, bf16[4,128,1024]{2,1,0:T(8,128)(2,1)} %wout_hbm.1), custom_call_target="tpu_custom_call" | custom-call | tf_op jit(solution)/shard_map/pallas_call | solution.py:310
  62.9 1.3 %copy.10 = f32[1,512]{1,0:T(1,128)} copy(f32[1,512]{1,0:T(1,128)} %shard_map.73) | data formatting | bytes 4096

commit v2 on v1

--- a/solution.py
+++ b/solution.py
@@ -9,6 +9,7 @@
 
 MESH = pl.DeviceIdType.MESH
 PIECES = 2
+STRIP = 128
 
 
 def silu(v):
@@ -17,7 +18,7 @@
 
 def kernel(
     chips, prefix_ref, ids_ref, key_hbm, value_hbm, table_hbm, w_hbm, wout_hbm, out_ref,
-    tab, ids_peer, ids_wide, picked, one_hot, emb, emb_peer, w, keys, values, wout, acc, gated,
+    tab, ids_peer, ids_wide, picked, one_hot, emb, emb_peer, w_raw, w_wide, w, keys, values, wout, acc, gated,
     gated_peer, halves, local_sem, z_send, z_recv, ids_sem, exch_send, exch_recv, wout_sem, tail_sem,
 ):
     grp, user, head = lax.axis_index("grp"), lax.axis_index("user"), lax.axis_index("head")
@@ -42,7 +43,7 @@
     )
     loads = [
         pltpu.make_async_copy(wout_hbm, wout.at[head], local_sem.at[1]),
-        pltpu.make_async_copy(w_hbm, w, local_sem.at[2]),
+        pltpu.make_async_copy(w_hbm, w_raw, local_sem.at[2]),
         pltpu.make_async_copy(key_hbm.at[0], keys, local_sem.at[3]),
         pltpu.make_async_copy(value_hbm.at[0], values, local_sem.at[4]),
     ]
@@ -144,8 +145,24 @@
             across(chip, part, 1 - core).wait_recv()
         pick(chip)
 
+    slots = heads * 4
+    strips = model // STRIP
+
+    def spread(i, carry):
+        start = pl.multiple_of(i * STRIP * slots, STRIP * slots)
+        w_wide[...] = w_raw[pl.ds(start, STRIP * slots)].astype(jnp.float32)
+        for j in range(slots):
+            w[pl.ds(pl.multiple_of(i * STRIP, STRIP), STRIP), j * head_size : (j + 1) * head_size] = (
+                w_wide[pl.ds(j, STRIP, stride=slots)].astype(jnp.bfloat16)
+            )
+        return carry
+
     take(z)
+    loads[1].wait()
     for distance in range(1, chips):
+        lax.fori_loop(
+            (distance - 1) * strips // (chips - 1), distance * strips // (chips - 1), spread, 0
+        )
         for part in range(PIECES):
 
             @pl.when(z - distance >= 0)
@@ -178,7 +195,7 @@
         (grp, sibling, head),
     )
     forward.start()
-    for load in loads[1:]:
+    for load in loads[2:]:
         load.wait()
 
     def weight(which, h):
@@ -323,6 +340,8 @@
             pltpu.VMEM((cand, rows), bf16),
             pltpu.VMEM((4, cand, width), bf16),
             pltpu.VMEM((cand, width), bf16),
+            pltpu.VMEM((model * heads * 4, head_size), bf16),
+            pltpu.VMEM((STRIP * heads * 4, head_size), f32),
             pltpu.VMEM((model, heads * 4 * head_size), bf16),
             pltpu.VMEM((prefix_most, here), bf16),
             pltpu.VMEM((prefix_most, here), bf16),
@@ -345,7 +364,7 @@
         ),
     )(
         prefix_len, cand_ids, key_cache, value_cache, item_table,
-        w_qkvu.reshape(model, heads * 4 * head_size), w_out,
+        w_qkvu.reshape(model * heads * 4, head_size), w_out,
     )
 
 

time: 64.5 us -> 58.1 us (0.901)
  local copies, waits for them, and re-layouts: 9.05 us -> 1.26 us
  Pallas kernels: 54.5 us -> 56 us
    reshape x1 -> x0, local copies, waits for them, and re-layouts: 7.8 us -> none  [fused_body(): w_qkvu.reshape(model, heads * 4 * head_size)]
    pallas_call x1, Pallas kernels: 54.5 us -> 56 us  [fused_body(): pl.pallas_call(functools.partial(kernel, chips), out_shape=jax.ShapeDtype...]
where the time goes in v2:
time: 58.1 us; the launch traced here: 57.9 us
  Pallas kernels  56 us (96%)
  local copies, waits for them, and re-layouts  1.26 us (2%)
  between operations  0.66 us (1%)
    pallas_call x1, Pallas kernels, fused_body(): pl.pallas_call(functools.partial(kernel, chips), out_shape=jax.ShapeDtype...  56 us
    unnamed x1, local copies, waits for them, and re-layouts  1.26 us

profile of v2, /device:TPU:0, one launch (start us, length us, event | category | flops | bytes accessed | tf_op | source)
XLA Modules:
  0.0 57.9 jit_solution(10947811483930987343)
XLA Ops:
  0.7 56.0 %shard_map.73 = f32[1,512]{1,0:T(1,128)} custom-call(s32[1]{0:T(128)S(6)} %copy.9.prefix_ref, s32[1,512]{1,0:T(1,128)} %ids_ref.1, bf16[1,512,512]{2,1,0:T(8,128)(2,1)} %key_hbm.1, bf16[1,512,512]{2,1,0:T(8,128)(2,1)} %value_hbm.1, bf16[512,1024]{1,0:T(8,128)(2,1)} %table_hbm.1, bf16[16384,128]{1,0:T(8,128)(2,1)} %bitcast.1, bf16[4,128,1024]{2,1,0:T(8,128)(2,1)} %wout_hbm.1), custom_call_target="tpu_custom_call" | custom-call | tf_op jit(solution)/shard_map/pallas_call | solution.py:327
  56.6 1.3 %copy.10 = f32[1,512]{1,0:T(1,128)} copy(f32[1,512]{1,0:T(1,128)} %shard_map.73) | data formatting | bytes 4096

commit v3 on v2

--- a/solution.py
+++ b/solution.py
@@ -114,36 +114,58 @@
     ids_copy.wait()
 
     lane = lax.broadcasted_iota(jnp.int32, (cand, 128), 1)
-    diagonal = lax.broadcasted_iota(jnp.int32, (cand, cand), 0) == lax.broadcasted_iota(
-        jnp.int32, (cand, cand), 1
-    )
+    down = lax.broadcasted_iota(jnp.int32, (cand, cand), 0)
+    diagonal = down == lax.broadcasted_iota(jnp.int32, (cand, cand), 1)
+    place_row = None
     for which, source in enumerate((ids_ref, ids_peer)):
-        column = jnp.sum(
-            jnp.where(diagonal, source[...].astype(jnp.float32), 0.0), axis=1, keepdims=True
+        ids = source[...]
+        chip_of = sum((ids >= k * 2 * rows).astype(jnp.int32) for k in range(1, chips))
+        key_row = (
+            jnp.abs(chip_of - z) * cand + lax.broadcasted_iota(jnp.int32, (1, cand), 1)
+        ).astype(jnp.float32)
+        key_column = jnp.sum(jnp.where(diagonal, key_row, 0.0), axis=1, keepdims=True)
+        place = jnp.sum(
+            jnp.where(key_column < key_row, 1.0, 0.0), axis=0, keepdims=True
         ).astype(jnp.int32)
-        ids_wide[which] = jnp.broadcast_to(column, (cand, 128))
+        ordered = jnp.sum(
+            jnp.where(place == down, ids.astype(jnp.float32), 0.0), axis=1, keepdims=True
+        ).astype(jnp.int32)
+        ids_wide[which] = jnp.broadcast_to(ordered, (cand, 128))
+        if which == 0:
+            place_row = place
     picked[...] = jnp.zeros_like(picked)
 
-    def pick(chip):
+    def mark(chip, low):
         def step(i, carry):
-            which, parity = i // 2, i % 2
-            shard = 2 * chip + parity
-            wide = ids_wide[which] - shard * rows
+            wide = ids_wide[i // 2, low:] - (2 * chip + i % 2) * rows
             for j in range(rows // 128):
-                one_hot[:, j * 128 : (j + 1) * 128] = jnp.where(
-                    wide == lane + j * 128, 1.0, 0.0
+                one_hot[i, low:, j * 128 : (j + 1) * 128] = jnp.where(
+                    wide == lane[low:] + j * 128, 1.0, 0.0
                 ).astype(jnp.bfloat16)
-            picked[which] += jnp.dot(
-                one_hot[...], tab[shard], preferred_element_type=jnp.float32
-            )
             return carry
 
         lax.fori_loop(0, 4, step, 0)
 
-    def take(chip):
+    def pick(chip, low):
+        def step(i, carry):
+            picked[i // 2, low:] += jnp.dot(
+                one_hot[i, low:], tab[2 * chip + i % 2], preferred_element_type=jnp.float32
+            )
+            return carry
+
+        lax.fori_loop(0, 4, step, 0)
+
+    def wait_sibling(chip):
         for part in range(PIECES):
             across(chip, part, 1 - core).wait_recv()
-        pick(chip)
+
+    def take(chip):
+        mark(chip, 0)
+        wait_sibling(chip)
+        pick(chip, 0)
+
+    def take_valid(chip):
+        pl.when(jnp.logical_and(chip >= 0, chip < chips))(lambda: take(chip))
 
     slots = heads * 4
     strips = model // STRIP
@@ -157,12 +179,50 @@
             )
         return carry
 
+    def weight(which, h):
+        return w[
+            pl.ds(pl.multiple_of(which * width, width), width),
+            pl.ds(pl.multiple_of(h * 4 * head_size, 4 * head_size), 4 * head_size),
+        ]
+
+    def embedded(which, start, count):
+        return emb[which, pl.ds(pl.multiple_of(start, count), count)]
+
+    def project(which, start, count, h):
+        return jnp.dot(
+            embedded(which, start, count), weight(which, h), preferred_element_type=jnp.float32
+        )
+
+    def swaps(r):
+        span = pl.ds(r * half, half)
+        mine, other = emb.at[quarter, span], emb_peer.at[span]
+        return [
+            remote(mine, mine, exch_send.at[r, 0], exch_recv.at[r, quarter], x_peer),
+            remote(other, mine, exch_send.at[r, 1], exch_recv.at[r, quarter], y_peer),
+            remote(other, mine, exch_send.at[r, 2], exch_recv.at[r, quarter], corner),
+        ]
+
+    def hand_out(r):
+        emb_peer[r * half : (r + 1) * half] = picked[1, r * half : (r + 1) * half].astype(jnp.bfloat16)
+        emb[quarter, r * half : (r + 1) * half] = picked[0, r * half : (r + 1) * half].astype(
+            jnp.bfloat16
+        )
+        for copy in swaps(r):
+            copy.start()
+
+        def first(h, carry):
+            acc[r, h] = project(quarter, r * half, half, h)
+            return carry
+
+        lax.fori_loop(0, heads, first, 0)
+
+    at_end = jnp.logical_or(z == 0, z == chips - 1)
+    inside = jnp.logical_and(z > 0, z < chips - 1)
+    near = 1 - 2 * jnp.minimum(z, 1)
     take(z)
     loads[1].wait()
+    lax.fori_loop(0, 3 * strips // 8, spread, 0)
     for distance in range(1, chips):
-        lax.fori_loop(
-            (distance - 1) * strips // (chips - 1), distance * strips // (chips - 1), spread, 0
-        )
         for part in range(PIECES):
 
             @pl.when(z - distance >= 0)
@@ -177,18 +237,32 @@
                 when(z > 0, lambda: along(z + distance, part, -1).start())
                 across(z + distance, part, core).start()
 
-        when(z - distance >= 0, lambda: take(z - distance))
-        when(z + distance < chips, lambda: take(z + distance))
-
-    emb[quarter] = picked[0].astype(jnp.bfloat16)
-    emb_peer[...] = picked[1].astype(jnp.bfloat16)
-    exchange = [
-        remote(emb.at[quarter], emb.at[quarter], exch_send.at[0], exch_recv.at[quarter], x_peer),
-        remote(emb_peer, emb.at[quarter], exch_send.at[1], exch_recv.at[quarter], y_peer),
-        remote(emb_peer, emb.at[quarter], exch_send.at[2], exch_recv.at[quarter], corner),
-    ]
-    for copy in exchange:
-        copy.start()
+            if part == 0:
+                if distance == 1:
+                    lax.fori_loop(3 * strips // 8, 5 * strips // 8, spread, 0)
+                else:
+                    take_valid(z - near * (distance - 1))
+                if distance == chips - 2:
+                    lax.fori_loop(6 * strips // 8, strips, spread, 0)
+                    when(inside, lambda: hand_out(0))
+            elif part == PIECES - 1:
+                if distance < chips - 1:
+                    take_valid(z + near * distance)
+                if distance == 1:
+                    lax.fori_loop(5 * strips // 8, 6 * strips // 8, spread, 0)
+                if distance == chips - 2:
+
+                    @pl.when(at_end)
+                    def _():
+                        hand_out(0)
+                        mark(z + near * (chips - 1), half)
+
+    @pl.when(at_end)
+    def _():
+        wait_sibling(z + near * (chips - 1))
+        pick(z + near * (chips - 1), half)
+
+    hand_out(1)
     to_peer.wait()
     forward = remote(
         wout_part(1 - head, core), wout_part(1 - head, core), wout_sem.at[2], wout_sem.at[3],
@@ -198,40 +272,12 @@
     for load in loads[2:]:
         load.wait()
 
-    def weight(which, h):
-        return w[
-            pl.ds(pl.multiple_of(which * width, width), width),
-            pl.ds(pl.multiple_of(h * 4 * head_size, 4 * head_size), 4 * head_size),
-        ]
-
-    def embedded(which, r):
-        return emb[which, pl.ds(pl.multiple_of(r * half, half), half)]
-
-    def project(which, r, h):
-        return jnp.dot(embedded(which, r), weight(which, h), preferred_element_type=jnp.float32)
-
-    def arrived(which):
-        remote(
-            emb.at[which], emb.at[which], exch_send.at[0], exch_recv.at[which], x_peer
-        ).wait_recv()
-
-    x_quarter, y_quarter = 2 * grp + 1 - head, 2 * (1 - grp) + head
-    corner_quarter = 2 * (1 - grp) + 1 - head
-
-    def first(i, carry):
-        acc[i // heads, i % heads] = project(quarter, i // heads, i % heads)
-        return carry
-
-    lax.fori_loop(0, 2 * heads, first, 0)
-    for which in (x_quarter, y_quarter):
-        arrived(which)
-
-        def add(i, carry):
-            acc[i // heads, i % heads] += project(which, i // heads, i % heads)
-            return carry
-
-        lax.fori_loop(0, 2 * heads, add, 0)
-    arrived(corner_quarter)
+    others = (2 * grp + 1 - head, 2 * (1 - grp) + head, 2 * (1 - grp) + 1 - head)
+
+    def arrived(r):
+        for which in others:
+            place = emb.at[which, pl.ds(r * half, half)]
+            remote(place, place, exch_send.at[r, 0], exch_recv.at[r, which], x_peer).wait_recv()
 
     length = prefix_ref[0]
     inverse = 1.0 / (length + 1).astype(jnp.float32)
@@ -239,9 +285,14 @@
     factor = jnp.where(in_prefix, inverse, 0.0)
     scale = head_size ** (-0.5)
 
-    def attend(r):
+    def attend(r, offset, count):
+        here_rows = pl.ds(pl.multiple_of(offset, count), count)
+
         def step(h, carry):
-            activated = silu(acc[r, h] + project(corner_quarter, r, h)).astype(jnp.bfloat16)
+            projected = acc[r, h, here_rows]
+            for which in others:
+                projected += project(which, r * half + offset, count, h)
+            activated = silu(projected).astype(jnp.bfloat16)
             query, own_key, own_value, gate = (
                 activated[:, j * head_size : (j + 1) * head_size] for j in range(4)
             )
@@ -257,18 +308,18 @@
             )
             attended += silu(own_dot * scale) * inverse * own_value.astype(jnp.float32)
             mean_square = jnp.mean(attended * attended, axis=1, keepdims=True)
-            gated[r, :, columns] = (
+            gated[r, here_rows, columns] = (
                 attended * lax.rsqrt(mean_square + 1e-06) * gate.astype(jnp.float32)
             ).astype(jnp.bfloat16)
             return carry
 
         lax.fori_loop(0, heads, step, 0)
 
-    attend(1 - head)
-    hand_over = remote(gated.at[1 - head], gated_peer, tail_sem.at[0], tail_sem.at[1], x_peer)
-    hand_over.start()
-    attend(head)
-    forward.wait()
+    eighth = half // 2
+
+    def hand_over(r):
+        place = gated.at[r, pl.ds(pl.multiple_of((1 - head) * eighth, eighth), eighth)]
+        return remote(place, gated_peer.at[r], tail_sem.at[r], tail_sem.at[2 + r], x_peer)
 
     def product(rows_here, group):
         return (
@@ -279,20 +330,35 @@
             .astype(jnp.float32)
         )
 
-    summed = product(gated[head], head)
-    hand_over.wait()
-    summed += product(gated_peer[...], 1 - head)
-    square = jnp.sum(summed * summed, axis=1, keepdims=True)
-    inner = sum(
-        jnp.sum(
-            summed[:, i * width : (i + 1) * width] * embedded(i, head).astype(jnp.float32),
-            axis=1, keepdims=True,
-        )
-        for i in range(model // width)
-    )
-    score = inner * model ** (-0.5) * lax.rsqrt(square / model + 1e-06)
-    halves[head] = jnp.sum(jnp.where(diagonal[:half, :half], score, 0.0), axis=0, keepdims=True)
-    last = remote(halves.at[head], halves.at[head], tail_sem.at[2], tail_sem.at[3], x_peer)
+    def finish(r):
+        offset = pl.multiple_of(head * eighth, eighth)
+        summed = product(gated[r, pl.ds(offset, eighth)], head)
+        hand_over(r).wait()
+        summed += product(gated_peer[r], 1 - head)
+        square = jnp.sum(summed * summed, axis=1, keepdims=True)
+        inner = sum(
+            jnp.sum(
+                summed[:, i * width : (i + 1) * width]
+                * embedded(i, r * half + offset, eighth).astype(jnp.float32),
+                axis=1, keepdims=True,
+            )
+            for i in range(model // width)
+        )
+        score = inner * model ** (-0.5) * lax.rsqrt(square / model + 1e-06)
+        slot = down[:eighth] + (r * half + offset)
+        return jnp.sum(jnp.where(place_row == slot, score, 0.0), axis=0, keepdims=True)
+
+    arrived(0)
+    attend(0, 0, half)
+    arrived(1)
+    hand_over(0).start()
+    attend(1, (1 - head) * eighth, eighth)
+    hand_over(1).start()
+    attend(1, head * eighth, eighth)
+    forward.wait()
+    early = finish(0)
+    halves[head] = early + finish(1)
+    last = remote(halves.at[head], halves.at[head], tail_sem.at[4], tail_sem.at[5], x_peer)
     last.start()
     for part in range(PIECES):
         for chip in range(chips):
@@ -306,11 +372,11 @@
                 when(chip >= z, lambda: along(chip, part, -1).wait_send())
 
             across(chip, part, core).wait_send()
-    for copy in exchange:
-        copy.wait_send()
+    for r in range(2):
+        for copy in swaps(r):
+            copy.wait_send()
     last.wait()
-    for i in range(2):
-        out_ref[:, i * half : (i + 1) * half] = halves[i]
+    out_ref[...] = halves[0] + halves[1]
 
 
 def fused_body(mesh, cand_ids, prefix_len, key_cache, value_cache, item_table, w_qkvu, w_out):
@@ -337,7 +403,7 @@
             pltpu.VMEM((1, cand), jnp.int32),
             pltpu.VMEM((2, cand, 128), jnp.int32),
             pltpu.VMEM((2, cand, width), f32),
-            pltpu.VMEM((cand, rows), bf16),
+            pltpu.VMEM((4, cand, rows), bf16),
             pltpu.VMEM((4, cand, width), bf16),
             pltpu.VMEM((cand, width), bf16),
             pltpu.VMEM((model * heads * 4, head_size), bf16),
@@ -348,16 +414,16 @@
             pltpu.VMEM((2, heads, head_size, model), bf16),
             pltpu.VMEM((2, heads, half, 4 * head_size), f32),
             pltpu.VMEM((2, half, here), bf16),
-            pltpu.VMEM((half, here), bf16),
-            pltpu.VMEM((2, 1, half), f32),
+            pltpu.VMEM((2, half // 2, here), bf16),
+            pltpu.VMEM((2, 1, cand), f32),
             pltpu.SemaphoreType.DMA((5,)),
             pltpu.SemaphoreType.DMA((3, chips, PIECES)),
             pltpu.SemaphoreType.DMA((2, chips, PIECES)),
             pltpu.SemaphoreType.DMA((2,)),
-            pltpu.SemaphoreType.DMA((3,)),
+            pltpu.SemaphoreType.DMA((2, 3)),
+            pltpu.SemaphoreType.DMA((2, 4)),
             pltpu.SemaphoreType.DMA((4,)),
-            pltpu.SemaphoreType.DMA((4,)),
-            pltpu.SemaphoreType.DMA((4,)),
+            pltpu.SemaphoreType.DMA((6,)),
         ],
         compiler_params=pltpu.CompilerParams(
             collective_id=0, has_side_effects=True, vmem_limit_bytes=60 * 1024 * 1024
@@ -370,7 +436,7 @@
 
 def fits_fused(mesh):
     shape = mesh.shape
-    return shape["grp"] == 2 and shape["head"] == 2 and shape["user"] % 2 == 0 and shape["user"] <= 8
+    return shape["grp"] == 2 and shape["head"] == 2 and shape["user"] == 8
 
 
 def fused(mesh):

time: 58.1 us -> 48.9 us (0.84)
  Pallas kernels: 56 us -> 46.8 us
    pallas_call x1, Pallas kernels: 56 us -> 46.8 us  [fused_body(): pl.pallas_call(functools.partial(kernel, chips), out_shape=jax.ShapeDtype...]
where the time goes in v3:
time: 48.9 us; the launch traced here: 48.7 us
  Pallas kernels  46.8 us (96%)
  local copies, waits for them, and re-layouts  1.26 us (3%)
  between operations  0.66 us (1%)
    pallas_call x1, Pallas kernels, fused_body(): pl.pallas_call(functools.partial(kernel, chips), out_shape=jax.ShapeDtype...  46.8 us
    unnamed x1, local copies, waits for them, and re-layouts  1.26 us

profile of v3, /device:TPU:0, one launch (start us, length us, event | category | flops | bytes accessed | tf_op | source)
XLA Modules:
  0.0 48.7 jit_solution(3123024963960203875)
XLA Ops:
  0.7 46.8 %shard_map.73 = f32[1,512]{1,0:T(1,128)} custom-call(s32[1]{0:T(128)S(6)} %copy.9.prefix_ref, s32[1,512]{1,0:T(1,128)} %ids_ref.1, bf16[1,512,512]{2,1,0:T(8,128)(2,1)} %key_hbm.1, bf16[1,512,512]{2,1,0:T(8,128)(2,1)} %value_hbm.1, bf16[512,1024]{1,0:T(8,128)(2,1)} %table_hbm.1, bf16[16384,128]{1,0:T(8,128)(2,1)} %bitcast.1, bf16[4,128,1024]{2,1,0:T(8,128)(2,1)} %wout_hbm.1), custom_call_target="tpu_custom_call" | custom-call | tf_op jit(solution)/shard_map/pallas_call | solution.py:393
  47.5 1.3 %copy.10 = f32[1,512]{1,0:T(1,128)} copy(f32[1,512]{1,0:T(1,128)} %shard_map.73) | data formatting | bytes 4096

commit v4 on v3

--- a/solution.py
+++ b/solution.py
@@ -8,7 +8,7 @@
 from jax.sharding import PartitionSpec as P
 
 MESH = pl.DeviceIdType.MESH
-PIECES = 2
+PIECES = 4
 STRIP = 128
 
 

time: 48.9 us -> 48.7 us (level)
  no operation moved by 1% of the time
where the time goes in v4:
time: 48.7 us; the launch traced here: 48.5 us
  Pallas kernels  46.6 us (96%)
  local copies, waits for them, and re-layouts  1.26 us (3%)
  between operations  0.66 us (1%)
    pallas_call x1, Pallas kernels, fused_body(): pl.pallas_call(functools.partial(kernel, chips), out_shape=jax.ShapeDtype...  46.6 us
    unnamed x1, local copies, waits for them, and re-layouts  1.26 us

profile of v4, /device:TPU:0, one launch (start us, length us, event | category | flops | bytes accessed | tf_op | source)
XLA Modules:
  0.0 48.5 jit_solution(247555445621143898)
XLA Ops:
  0.7 46.6 %shard_map.73 = f32[1,512]{1,0:T(1,128)} custom-call(s32[1]{0:T(128)S(6)} %copy.9.prefix_ref, s32[1,512]{1,0:T(1,128)} %ids_ref.1, bf16[1,512,512]{2,1,0:T(8,128)(2,1)} %key_hbm.1, bf16[1,512,512]{2,1,0:T(8,128)(2,1)} %value_hbm.1, bf16[512,1024]{1,0:T(8,128)(2,1)} %table_hbm.1, bf16[16384,128]{1,0:T(8,128)(2,1)} %bitcast.1, bf16[4,128,1024]{2,1,0:T(8,128)(2,1)} %wout_hbm.1), custom_call_target="tpu_custom_call" | custom-call | tf_op jit(solution)/shard_map/pallas_call | solution.py:393
  47.2 1.3 %copy.10 = f32[1,512]{1,0:T(1,128)} copy(f32[1,512]{1,0:T(1,128)} %shard_map.73) | data formatting | bytes 4096
